TPU v7x, 512 devices: a whole 4x4x16 slice. The times are simulated.
512 devices in a mesh: pair: 16 (over y, x), virt: 32 (over z, core).
Axes of the slice: x: 4, y: 4, z: 16, core: 2. Of those that a mesh axis runs over, the one named last changes fastest.
Arguments:
- density_row_blocks: bfloat16 [640, 512, 2744], P('pair', 'virt'), may hold values from -6 to 6
- vir_left: bfloat16 [512, 2744], P('virt'), may hold values from -0.01171875 to 0.01171875
- vir_right: bfloat16 [512, 2744], P('virt'), may hold values from -0.109375 to 0.109375
- orb_energy: bfloat16 [512], P('virt'), may hold values from 0.5 to 3
- state_energy: float32 [8], replicated, may hold values from -1 to -0.1
- bra_ket_states: int32 [640, 2], P('pair'), may hold values from 0 to 7
- row_block_starts: int32 [640], P('pair'), may hold values from 0 to 2232
Outputs:
- slot_couplings: float32 [640], P('pair')
- heff: float32 [8, 8], replicated
All inputs are finite; a program needn't handle non-finite values.
Results may differ from a plain program's by a relative error of at most 0.0003.
Values may be sent and summed in bfloat16 or wider, within the bound.
A program may use at most 64 MiB of HBM per device.

v0:
```python
import jax
import jax.numpy as jnp
from jax import lax
from jax.sharding import PartitionSpec as P


def in_one_piece(arrays, axis, dim, along):
    columns = [a.reshape(*a.shape[:along], -1) for a in arrays]
    both = jnp.concatenate(columns, axis=along)
    out, at, done = (lax.all_gather(both, axis, axis=dim, tiled=True), 0, [])
    for a, column in zip(arrays, columns):
        slab = out[..., at : at + column.shape[along]]
        done.append(slab.reshape(*slab.shape[:along], *a.shape[along:]))
        at += column.shape[along]
    return tuple(done)


def sent_to_all(x, axis):
    size = lax.axis_size(axis)
    return lax.all_to_all(jnp.broadcast_to(x[None], (size, *x.shape)), axis, 0, 0, tiled=True)


def over_copies(x, axis):
    return sent_to_all(x, axis).sum(axis=0)


def local(
    density_row_blocks,
    vir_left,
    vir_right,
    orb_energy,
    state_energy,
    bra_ket_states,
    row_block_starts,
):
    slots, rows, ntrip = density_row_blocks.shape
    nstate = state_energy.shape[0]
    virt_index = lax.axis_index("virt")
    positions = (
        row_block_starts[:, None] + virt_index * rows + jnp.arange(rows, dtype=jnp.int32)[None, :]
    )
    positions = positions.reshape(slots * rows)
    flat_rdm = density_row_blocks.reshape(slots * rows, ntrip)
    states = jnp.arange(nstate, dtype=jnp.int32)
    first = (bra_ket_states[:, 0:1] == states[None, :]).astype(jnp.float32)
    second = (bra_ket_states[:, 1:2] == states[None, :]).astype(jnp.float32)
    shift = jnp.dot(first + second, state_energy, precision=lax.Precision.HIGHEST)
    pieces = in_one_piece((vir_left, vir_right, orb_energy), "virt", 0, 1)
    columns = jnp.take(pieces[0], positions, axis=1)
    right_piece = pieces[1]
    count = right_piece.shape[0]
    contracted = lax.dot_general(
        right_piece, flat_rdm, (((1,), (1,)), ((), ())), preferred_element_type=jnp.float32
    )
    inverse = 1.0 / (pieces[2].astype(jnp.float32)[:, None] - shift[None, :])
    product = columns.astype(jnp.float32).reshape(count, slots, rows) * contracted.reshape(
        count, slots, rows
    )
    partial_sums = jnp.sum(jnp.sum(product, axis=2) * inverse, axis=0)
    couplings = over_copies(partial_sums, "virt")
    local_sum = jnp.dot(first.T, couplings[:, None] * second, precision=lax.Precision.HIGHEST)
    coupling_sum = over_copies(local_sum, "pair")
    heff = jnp.diag(state_energy) + 0.5 * (coupling_sum + coupling_sum.T)
    return (couplings, heff)


def solution(mesh):
    placed = (
        P("pair", "virt", None),
        P("virt", None),
        P("virt", None),
        P("virt"),
        P(),
        P("pair", None),
        P("pair"),
    )
    return jax.shard_map(
        local, mesh=mesh, in_specs=placed, out_specs=(P("pair"), P()), check_vma=False
    )
```

profile of v0, /device:TPU:1, one launch (start us, length us, event | category | flops | bytes accessed | tf_op | source)
XLA Modules:
  0.0 148.1 jit_solution(17433982153595554151)
XLA Ops:
  7.2 0.0 all-gather.2.cloned.1.call-start
  7.2 0.7 copy.49
  8.0 1.8 %concatenate.3 = bf16[16,5489]{1,0:T(8,128)(2,1)} concatenate(bf16[16,2744]{1,0:T(8,128)(2,1)} %param.8, bf16[16,2744]{1,0:T(8,128)(2,1)} %param.9, bf16[16,1]{1,0:T(8,128)(2,1)S(1)} %copy.49), dimensions={1} | concatenate | bytes 351296 | tf_op jit(solution)/shard_map/concatenate | solution.py:9
  9.7 0.0 all-gather.2.cloned.1.call-update
  9.7 0.7 broadcast_add_fusion
  10.4 0.1 copy.51
  10.5 0.1 add.72
  10.6 0.8 slice_bitcast_fusion.7
  11.4 0.9 convolution_bitcast_fusion
  12.3 78.8 %all-gather.2.cloned.1.call-done = bf16[512,5489]{1,0:T(8,128)(2,1)} async-done(((bf16[16,5489]{1,0:T(8,128)(2,1)}), bf16[512,5489]{1,0:T(8,128)(2,1)}) %all-gather.2.cloned.1.call-update) | async-done | bytes 5620752 | tf_op jit(solution)/shard_map/all_gather | solution.py:10
  91.1 3.6 %slice.22 = bf16[512,2744]{1,0:T(8,128)(2,1)} slice(bf16[512,5489]{1,0:T(8,128)(2,1)} %all-gather.2.cloned.1.call-done), slice={[0:512], [0:2744]} | slice | bytes 5619712 | tf_op jit(solution)/shard_map/slice | solution.py:12
  94.7 3.4 %copy.59 = bf16[512,2744]{0,1:T(8,128)(2,1)S(1)} copy(bf16[512,2744]{1,0:T(8,128)(2,1)} %slice.22) | data formatting | bytes 5619712
  98.1 2.8 %gather_fusion = bf16[640,512]{1,0:T(8,128)(2,1)S(1)} fusion(bf16[512,2744]{0,1:T(8,128)(2,1)S(1)} %copy.59, s32[1024]{0:T(1024)S(1)} %pad_clamp_fusion), kind=kCustom, calls=%fused_computation | custom fusion | bytes 1313280 | tf_op jit(solution)/shard_map/jit(_take)/gather | solution.py:49
  100.9 1.1 convert_reduce_fusion
  102.0 0.0 copy-start
  102.0 5.5 %fusion.5 = f32[512,40]{0,1:T(8,128)S(1)} fusion(bf16[40,16,2744]{2,1,0:T(8,128)(2,1)} %param.7, bf16[512,5489]{1,0:T(8,128)(2,1)} %all-gather.2.cloned.1.call-done, bf16[512,40,16]{0,2,1:T(8,128)(2,1)S(1)} %bitcast.28, pred[40,16]{0,1:T(8,128)(4,1)S(1)} %compare_and_fusion), kind=kOutput, calls=%fused_computation.5 | convolution fusion | flops 1799598080 | bytes 7225984 | tf_op jit(solution)/shard_map/dot_general | solution.py:52
  107.5 0.2 multiply_reduce_fusion
  107.7 19.7 %all_to_all.11 = f32[32,1,40]{2,1,0:T(1,128)S(1)} all-to-all(f32[32,1,40]{2,1,0:T(1,128)S(1)} %broadcast_in_dim.49), channel_id=1, replica_groups=mesh['pair'=16,'virt'=32] {'virt'}, dimensions={0} | all-to-all | bytes 10240 | tf_op jit(solution)/shard_map/all_to_all | solution.py:20
  127.4 0.0 copy-start.1
  127.4 0.3 fusion.8
  127.7 12.9 %all_to_all.12 = f32[16,8,8]{2,1,0:T(8,128)S(1)} all-to-all(f32[16,8,8]{2,1,0:T(8,128)S(1)} %broadcast_in_dim.52), channel_id=1, replica_groups=mesh['pair'=16,'virt'=32] {'pair'}, dimensions={0} | all-to-all | bytes 8192 | tf_op jit(solution)/shard_map/all_to_all | solution.py:20
  140.5 0.1 copy.57
  140.6 0.0 copy-done
  140.6 0.7 fusion.20
  141.3 0.0 copy-done.1
  (8 shorter events, 0.1 us)
Async XLA Ops:
  7.2 83.9 %all-gather.2.cloned.1.call-start = ((), (), s32[]{:S(2)}) async-start(), calls=%async_computation.2 | async-start | bytes 5812224 | tf_op jit(solution)/shard_map/all_gather | solution.py:10
  102.0 38.6 %copy-start = (f32[8]{0:T(128)S(1)}, f32[8]{0:T(128)}, u32[]{:S(2)}) copy-start(f32[8]{0:T(128)} %param.11) | copy-start | bytes 100
  127.4 13.9 %copy-start.1 = (f32[40]{0:T(128)}, f32[40]{0:T(128)S(1)}, u32[]{:S(2)}) copy-start(f32[40]{0:T(128)S(1)} %reduce_sum.38) | copy-start | bytes 484
Sparse Core Ops, SparseCore 0:
  10.1 80.9 all-gather.1
where the time goes:
time: 148 us
  waiting for transfers between devices  78.9 us (53%)
  blocking collectives  32.6 us (22%)
  between operations  14.1 us (10%)
  local copies, waits for them, and re-layouts  13.3 us (9%)
  matrix products  6.57 us (4%)
  other arithmetic  2.72 us (2%)
    all_gather x1, waiting for transfers between devices, in_one_piece(): out, at, done = (lax.all_gather(both, axis, axis=dim, tiled=True), 0, [])  78.8 us
    all_to_all x2, blocking collectives, sent_to_all(): lax.all_to_all(jnp.broadcast_to(x[None], (size, *x.shape)), axis, 0, 0, t...  32.6 us
    dot_general x1, matrix products, local(): lax.dot_general(right_piece, flat_rdm, (((1,), (1,)), ((), ())), preferre...  5.46 us
    slice x1, local copies, waits for them, and re-layouts, in_one_piece(): slab = out[..., at:at + column.shape[along]]  3.59 us
    unnamed x5, local copies, waits for them, and re-layouts  3.38 us
  transfers between devices with their start and end apart: 1, of which 1 were waited for; matrix products, arithmetic and copies ran while one was open for 2% of the time, Pallas kernels for 0%

commit v1 on v0

v1 whole, which is shorter than its diff:
```python
import jax
import jax.numpy as jnp
from jax import lax
from jax.experimental import pallas as pl
from jax.experimental.pallas import tpu as pltpu
from jax.sharding import PartitionSpec as P

MESH = pl.DeviceIdType.MESH
F32, BF16, I32 = jnp.float32, jnp.bfloat16, jnp.int32
SIDE = 4
LONG = 16
LANES = 128
OWN = 12


def nt(a, b):
    return lax.dot_general(a, b, (((1,), (1,)), ((), ())), preferred_element_type=F32)


def kernel(
    starts, states, levels, states_v, energy, left_hbm, right_hbm, dens_hbm,
    coup_ref, heff_ref,
    lv, rv, dens, pick, gp, gz, acc_l, acc_t, part, cbuf, hbuf,
    load_sem, dens_send, dens_recv,
    zs_send, zs_recv, zp_send, zp_recv, p1_send, p1_recv, p2_send, p2_recv,
    c_send, c_recv, h_send, h_recv,
):
    slots, rows, ntrip = dens_hbm.shape
    tiles = -(-ntrip // LANES)
    wide = tiles * LANES
    full = ntrip // LANES * LANES
    rest = ntrip - full
    pair = lax.axis_index("pair")
    virt = lax.axis_index("virt")
    y, x = pair // SIDE, lax.rem(pair, SIDE)
    z, core = virt // 2, lax.rem(virt, 2)

    def at(yy, xx, zz, cc):
        return (yy * SIDE + xx, zz * 2 + cc)

    def turn(v, by, n):
        return lax.rem(v + by + n, n)

    loads = [
        pltpu.make_async_copy(left_hbm, lv, load_sem.at[0]),
        pltpu.make_async_copy(right_hbm, rv, load_sem.at[1]),
        pltpu.make_async_copy(dens_hbm, dens.at[core], load_sem.at[2]),
    ]
    for c in loads:
        c.start()
    barrier = pltpu.get_barrier_semaphore()
    up = at(y, x, turn(z, 1, LONG), core)
    down = at(y, x, turn(z, -1, LONG), core)
    other = at(y, x, z, 1 - core)
    near = [up, down, other]
    near += [at(y, turn(x, j, SIDE), z, core) for j in (1, 2, 3)]
    near += [at(turn(y, j, SIDE), x, z, core) for j in (1, 2, 3)]
    for d in near:
        pl.semaphore_signal(barrier, inc=1, device_id=d, device_id_type=MESH)

    loads[0].wait()
    loads[1].wait()
    eye = lax.broadcasted_iota(I32, (rows, rows), 0) == lax.broadcasted_iota(I32, (rows, rows), 1)
    ecol = jnp.sum(jnp.where(eye, energy[...], 0.0), axis=1, keepdims=True)
    col = lax.broadcasted_iota(I32, (rows, LANES), 1)
    pad = jnp.zeros((rows, LANES - rest), F32)

    def put(t, value):
        if t < 2 * SIDE * SIDE:
            gp[0, t // (2 * SIDE), t // 2 % SIDE, t % 2] = value
        else:
            gz[0, t - 2 * SIDE * SIDE] = value

    for src, base in ((lv, 0), (rv, tiles)):
        for t in range(tiles - 1):
            put(base + t, src[:, t * LANES : (t + 1) * LANES])
        last = jnp.concatenate([src[:, full:ntrip].astype(F32), pad], axis=1)
        if base == 0:
            last = jnp.where(col == rest, ecol, last)
        put(base + tiles - 1, last.astype(BF16))

    pl.semaphore_wait(barrier, len(near))

    def send(src, dst, ssem, rsem, dev):
        return pltpu.make_async_remote_copy(
            src_ref=src, dst_ref=dst, send_sem=ssem, recv_sem=rsem, device_id=dev, device_id_type=MESH
        )

    def slot_of(way, k):
        return k if way == 0 else jnp.where(k == 0, 0, k + 8)

    def stripe(way, k):
        dst = slot_of(way, k + 1)
        return send(
            gp.at[slot_of(way, k), y, x], gp.at[dst, y, x],
            zs_send.at[dst], zs_recv.at[dst], up if way == 0 else down,
        )

    def lane(way, k):
        dst = slot_of(way, k + 1)
        return send(
            gz.at[slot_of(way, k)], gz.at[dst],
            zp_send.at[dst], zp_recv.at[dst], up if way == 0 else down,
        )

    def first(way, k, j):
        s = slot_of(way, k)
        dev = at(y, turn(x, j, SIDE), z, core) if way == 0 else at(turn(y, j, SIDE), x, z, core)
        return send(gp.at[s, y, x], gp.at[s, y, x], p1_send.at[s, j - 1], p1_recv.at[s, j - 1], dev)

    def second(way, k, j):
        s = slot_of(way, k)
        if way == 0:
            ref, dev = gp.at[s, y], at(turn(y, j, SIDE), x, z, core)
        else:
            ref, dev = gp.at[s, :, x], at(y, turn(x, j, SIDE), z, core)
        return send(ref, ref, p2_send.at[s, j - 1], p2_recv.at[s, j - 1], dev)

    def first_in(way, k, j):
        s = slot_of(way, k)
        ref = gp.at[s, y, turn(x, -j, SIDE)] if way == 0 else gp.at[s, turn(y, -j, SIDE), x]
        return send(ref, ref, p1_send.at[s, j - 1], p1_recv.at[s, j - 1], other)

    def second_in(way, k, j):
        s = slot_of(way, k)
        ref = gp.at[s, turn(y, -j, SIDE)] if way == 0 else gp.at[s, :, turn(x, -j, SIDE)]
        return send(ref, ref, p2_send.at[s, j - 1], p2_recv.at[s, j - 1], other)

    for way in (0, 1):
        stripe(way, 0).start()
    for way in (0, 1):
        lane(way, 0).start()
    give = send(dens_hbm, dens.at[core], dens_send.at[0], dens_recv.at[0], other)
    give.start()

    ahead = lax.broadcasted_iota(I32, (rows, wide), 1) - lax.broadcasted_iota(I32, (rows, wide), 0)

    def fill(i, carry):
        at_col = starts[lax.rem(i, slots)] + rows * (2 * z + i // slots)
        pick[i] = jnp.where(ahead == at_col, 1.0, 0.0).astype(BF16)
        return carry

    lax.fori_loop(0, 2 * slots, fill, 0)
    pick[2 * slots] = jnp.where(ahead == ntrip, 1.0, 0.0).astype(BF16)

    def step(k, carry):
        for way in (0, 1):
            stripe(way, k - 1).wait_recv()
            if way == 0:
                stripe(way, k).start()
            else:
                @pl.when(k < 7)
                def _():
                    stripe(1, k).start()
            for j in (2, 1, 3):
                first(way, k, j).start()
        for way in (0, 1):
            lane(way, k - 1).wait_recv()
            if way == 0:
                lane(way, k).start()
            else:
                @pl.when(k < 7)
                def _():
                    lane(1, k).start()

        @pl.when(k > 1)
        def _():
            for way in (0, 1):
                for j in (1, 2, 3):
                    first_in(way, k - 1, j).wait_recv()
                for j in (2, 1, 3):
                    second(way, k - 1, j).start()
        return carry

    lax.fori_loop(1, 8, step, 0)
    stripe(0, 7).wait_recv()
    for j in (2, 1, 3):
        first(0, 8, j).start()
    for way, k in ((0, 7), (1, 7), (0, 8)):
        for j in (1, 2, 3):
            first_in(way, k, j).wait_recv()
        for j in (2, 1, 3):
            second(way, k, j).start()
    lane(0, 7).wait_recv()

    def arrived(k, carry):
        for way in (0, 1):
            for j in (1, 2, 3):
                second_in(way, k, j).wait_recv()
        return carry

    lax.fori_loop(1, 8, arrived, 0)
    for j in (1, 2, 3):
        second_in(0, 8, j).wait_recv()
    loads[2].wait()
    give.wait_recv()

    def two(t):
        halves = []
        for u in (t, t + 1):
            if u < 2 * SIDE * SIDE:
                v = gp[:, u // (2 * SIDE), u // 2 % SIDE, u % 2]
            else:
                v = gz[:, u - 2 * SIDE * SIDE]
            halves.append(v.reshape(LONG * rows, LANES))
        return jnp.concatenate(halves, axis=1)

    for m in range(tiles // 2):
        cols = slice(2 * m * LANES, 2 * (m + 1) * LANES)
        got = nt(pick[:, :, cols].reshape((2 * slots + 1) * rows, 2 * LANES), two(2 * m))
        if m == 0:
            acc_l[...] = got
        else:
            acc_l[...] += got
    for m in range(tiles // 2):
        if m < tiles // 2 - 1:
            d = dens[:, :, :, 2 * m * LANES : 2 * (m + 1) * LANES].reshape(2 * slots * rows, 2 * LANES)
        else:
            d = dens[:, :, :, 2 * m * LANES : ntrip].reshape(2 * slots * rows, ntrip - 2 * m * LANES)
            d = jnp.concatenate([d, jnp.zeros((2 * slots * rows, wide - ntrip), BF16)], axis=1)
        got = nt(d, two(tiles + 2 * m))
        if m == 0:
            acc_t[...] = got
        else:
            acc_t[...] += got

    erow = jnp.broadcast_to(acc_l[2 * slots * rows : 2 * slots * rows + 1, :], (8, LONG * rows))

    def couple(s, carry):
        shift = levels[states[0, s]] + levels[states[1, s]]
        inv = 1.0 / (erow - shift)
        p = pl.multiple_of(s * rows, rows)
        q = pl.multiple_of((s + slots) * rows, rows)
        v = acc_l[pl.ds(p, rows), :] * acc_t[pl.ds(p, rows), :]
        v += acc_l[pl.ds(q, rows), :] * acc_t[pl.ds(q, rows), :]
        w = (v[:8] + v[8:]) * inv
        part[s] = w[:, :LANES] + w[:, LANES:]
        return carry

    lax.fori_loop(0, slots, couple, 0, unroll=4)
    ccol = jnp.sum(jnp.sum(part[...], axis=1), axis=1, keepdims=True)
    diag = lax.broadcasted_iota(I32, (slots, LANES), 0) == lax.broadcasted_iota(I32, (slots, LANES), 1)
    cbuf[virt] = jnp.sum(jnp.where(diag, ccol, 0.0), axis=0, keepdims=True)

    nv = 2 * LONG

    def couplings(j):
        dev = (pair, lax.rem(virt + j, nv))
        return send(cbuf.at[virt], cbuf.at[virt], c_send.at[j], c_recv.at[j], dev)

    def couplings_in(j):
        ref = cbuf.at[lax.rem(virt + nv - j, nv)]
        return send(ref, ref, c_send.at[j], c_recv.at[j], other)

    def go(j, carry):
        couplings(j).start()
        return carry

    def come(j, carry):
        couplings_in(j).wait_recv()
        return carry

    lax.fori_loop(1, nv, go, 0)
    lax.fori_loop(1, nv, come, 0)
    total = jnp.sum(cbuf[...], axis=0)
    coup_ref[...] = total[:, :slots]

    c = total[:, :slots]
    bra, ket = states_v[0:1, :], states_v[1:2, :]
    state = lax.broadcasted_iota(I32, (8, slots), 0)
    side = lax.broadcasted_iota(I32, (8, LANES), 1)
    by_bra = jnp.where(state == bra, c, 0.0)
    by_ket = jnp.where(state == ket, c, 0.0)
    local = jnp.zeros((8, LANES), F32)
    for n in range(8):
        sums = jnp.sum(
            jnp.where(ket == n, by_bra, 0.0) + jnp.where(bra == n, by_ket, 0.0), axis=1, keepdims=True
        )
        local = jnp.where(side == n, sums, local)
    hbuf[pair] = local
    np_ = SIDE * SIDE

    def plane(j):
        dev = (lax.rem(pair + j, np_), virt)
        return send(hbuf.at[pair], hbuf.at[pair], h_send.at[j], h_recv.at[j], dev)

    def plane_in(j):
        ref = hbuf.at[lax.rem(pair + np_ - j, np_)]
        return send(ref, ref, h_send.at[j], h_recv.at[j], other)

    for j in range(1, np_):
        plane(j).start()

    give.wait_send()

    def left(k, carry):
        for way in (0, 1):
            stripe(way, k - 1).wait_send()
            lane(way, k - 1).wait_send()
            for j in (1, 2, 3):
                first(way, k, j).wait_send()
                second(way, k, j).wait_send()
        return carry

    lax.fori_loop(1, 8, left, 0)
    stripe(0, 7).wait_send()
    lane(0, 7).wait_send()
    for j in (1, 2, 3):
        first(0, 8, j).wait_send()
        second(0, 8, j).wait_send()

    def gone(j, carry):
        couplings(j).wait_send()
        return carry

    lax.fori_loop(1, nv, gone, 0)

    for j in range(1, np_):
        plane_in(j).wait_recv()
    square = jnp.sum(hbuf[...], axis=0)[:, :8]
    one = lax.broadcasted_iota(I32, (8, 8), 0)
    two_ = lax.broadcasted_iota(I32, (8, 8), 1)
    out = 0.5 * square
    for n in range(8):
        out += jnp.where((one == n) & (two_ == n), levels[n], 0.0)
    heff_ref[...] = out
    for j in range(1, np_):
        plane(j).wait_send()


def local(density, left, right, energy, levels, states, starts):
    slots, rows, ntrip = density.shape
    n = rows * LONG
    wide = -(-ntrip // LANES) * LANES
    smem, vmem, hbm = (pl.BlockSpec(memory_space=m) for m in (pltpu.SMEM, pltpu.VMEM, pl.ANY))
    dma, reg = pltpu.SemaphoreType.DMA, pltpu.SemaphoreType.REGULAR
    pair_states = states.T
    couplings, heff = pl.pallas_call(
        kernel,
        out_shape=(jax.ShapeDtypeStruct((1, slots), F32), jax.ShapeDtypeStruct((8, 8), F32)),
        in_specs=[smem, smem, smem, vmem, vmem, hbm, hbm, hbm],
        out_specs=(vmem, vmem),
        scratch_shapes=[
            pltpu.VMEM((rows, ntrip), BF16),
            pltpu.VMEM((rows, ntrip), BF16),
            pltpu.VMEM((2, slots, rows, ntrip), BF16),
            pltpu.VMEM((2 * slots + 1, rows, wide), BF16),
            pltpu.VMEM((LONG, SIDE, SIDE, 2, rows, LANES), BF16),
            pltpu.VMEM((LONG, OWN, rows, LANES), BF16),
            pltpu.VMEM(((2 * slots + 1) * rows, n), F32),
            pltpu.VMEM((2 * slots * rows, n), F32),
            pltpu.VMEM((slots, 8, LANES), F32),
            pltpu.VMEM((2 * LONG, 1, LANES), F32),
            pltpu.VMEM((SIDE * SIDE, 8, LANES), F32),
            dma((3,)), dma((1,)), dma((1,)),
            dma((LONG,)), dma((LONG,)), dma((LONG,)), dma((LONG,)),
            dma((LONG, 3)), dma((LONG, 3)), dma((LONG, 3)), dma((LONG, 3)),
            dma((2 * LONG,)), dma((2 * LONG,)), dma((SIDE * SIDE,)), dma((SIDE * SIDE,)),
        ],
        compiler_params=pltpu.CompilerParams(
            collective_id=0, has_side_effects=True, vmem_limit_bytes=52 * 1024 * 1024
        ),
    )(
        starts, pair_states, levels, pair_states, energy.astype(F32).reshape(1, rows),
        left, right, density,
    )
    return couplings.reshape(slots), heff


def solution(mesh):
    placed = (
        P("pair", "virt", None),
        P("virt", None),
        P("virt", None),
        P("virt"),
        P(),
        P("pair", None),
        P("pair"),
    )
    return jax.shard_map(
        local, mesh=mesh, in_specs=placed, out_specs=(P("pair"), P()), check_vma=False
    )
```

time: 148 us -> 71.7 us (0.48)
  waiting for transfers between devices: 78.9 us -> 0 us
  Pallas kernels: 0 us -> 65.3 us
  blocking collectives: 32.6 us -> 0 us
  between operations: 14.1 us -> 0.64 us
  local copies, waits for them, and re-layouts: 13.3 us -> 4.87 us
  matrix products: 6.57 us -> 0 us
  other arithmetic: 2.72 us -> 0.66 us
    all_gather x1 -> x0, waiting for transfers between devices: 78.8 us -> none  [in_one_piece(): out, at, done = (lax.all_gather(both, axis, axis=dim, tiled=True), 0, [])]
    pallas_call x0 -> x1, Pallas kernels: none -> 65.3 us  [local(): pl.pallas_call(kernel, out_shape=(jax.ShapeDtypeStruct((1, slots), F32),...]
    all_to_all x2 -> x0, blocking collectives: 32.6 us -> none  [sent_to_all(): lax.all_to_all(jnp.broadcast_to(x[None], (size, *x.shape)), axis, 0, 0, t...]
    dot_general x3 -> x0, matrix products: 6.57 us -> none  [the longest x1 5.46 us: local(): lax.dot_general(right_piece, flat_rdm, (((1,), (1,)), ((), ())), preferre...]
    slice x1 -> x0, local copies, waits for them, and re-layouts: 3.59 us -> none  [in_one_piece(): slab = out[..., at:at + column.shape[along]]]
    gather x1 -> x0, local copies, waits for them, and re-layouts: 2.79 us -> none  [local(): columns = jnp.take(pieces[0], positions, axis=1)]
    concatenate x1 -> x0, local copies, waits for them, and re-layouts: 1.75 us -> none  [in_one_piece(): both = jnp.concatenate(columns, axis=along)]
    unnamed x5 -> x12, local copies, waits for them, and re-layouts: 3.38 us -> 4.87 us
  transfers between devices with their start and end apart: 1 -> 0, of which waited for: 1 -> 0; matrix products, arithmetic and copies ran while one was open for 2% -> 0% of each run, Pallas kernels for 0% -> 0%
where the time goes in v1:
time: 71.7 us; the launch traced here: 71.5 us
  Pallas kernels  65.3 us (91%)
  local copies, waits for them, and re-layouts  4.87 us (7%)
    pallas_call x1, Pallas kernels, local(): pl.pallas_call(kernel, out_shape=(jax.ShapeDtypeStruct((1, slots), F32),...  65.3 us
    unnamed x12, local copies, waits for them, and re-layouts  4.87 us

profile of v1, /device:TPU:1, one launch (start us, length us, event | category | flops | bytes accessed | tf_op | source)
XLA Modules:
  0.0 71.5 jit_solution(15052839743671494481)
XLA Ops:
  0.6 0.7 bitcast_convert_fusion.energy
  1.3 0.0 copy-start
  1.3 0.9 %copy-done = bf16[16,2744]{1,0:T(8,128)(2,1)S(1)} copy-done((bf16[16,2744]{1,0:T(8,128)(2,1)S(1)}, bf16[16,2744]{1,0:T(8,128)(2,1)}, u32[]{:S(2)}) %copy-start) | copy-done | bytes 87832
  2.2 0.0 copy-start.1
  2.2 0.9 %copy-done.1 = bf16[16,2744]{1,0:T(8,128)(2,1)S(1)} copy-done((bf16[16,2744]{1,0:T(8,128)(2,1)S(1)}, bf16[16,2744]{1,0:T(8,128)(2,1)}, u32[]{:S(2)}) %copy-start.1) | copy-done | bytes 87832
  3.1 0.0 copy-start.2
  3.1 0.7 copy-done.2
  3.7 0.0 copy-start.3
  3.8 0.7 copy-done.3
  4.4 0.0 copy-start.4
  4.4 0.7 copy-done.4
  5.1 65.3 %shard_map.86 = (f32[1,40]{1,0:T(1,128)S(1)}, f32[8,8]{1,0:T(8,128)S(1)}) custom-call(s32[40]{0:T(128)S(1)} %copy-done.3, s32[2,40]{1,0:T(2,128)S(1)} %bitcast.5, f32[8]{0:T(128)S(1)} %copy-done.4, s32[2,40]{1,0:T(2,128)S(1)} %bitcast.6, f32[1,16]{1,0:T(1,128)S(1)} %bitcast_convert_fusion.energy, bf16[16,2744]{1,0:T(8,128)(2,1)S(1)} %copy-done, ...), custom_call_target="tpu_custom_call" | custom-call | tf_op jit(solution)/shard_map/pallas_call | solution.py:338
  70.4 0.5 copy.11
  70.9 0.6 copy.12
Async XLA Ops:
  1.3 0.9 %copy-start = (bf16[16,2744]{1,0:T(8,128)(2,1)S(1)}, bf16[16,2744]{1,0:T(8,128)(2,1)}, u32[]{:S(2)}) copy-start(bf16[16,2744]{1,0:T(8,128)(2,1)} %left_hbm.1) | copy-start | bytes 263428
  2.2 0.9 %copy-start.1 = (bf16[16,2744]{1,0:T(8,128)(2,1)S(1)}, bf16[16,2744]{1,0:T(8,128)(2,1)}, u32[]{:S(2)}) copy-start(bf16[16,2744]{1,0:T(8,128)(2,1)} %right_hbm.1) | copy-start | bytes 263428
  3.1 0.7 copy-start.2
  3.7 0.7 copy-start.3
  4.4 0.7 copy-start.4

commit v2 on v1

--- a/solution.py
+++ b/solution.py
@@ -11,6 +11,8 @@
 LONG = 16
 LANES = 128
 OWN = 12
+CUTS = 3
+GIVES = 8
 
 
 def nt(a, b):
@@ -18,9 +20,9 @@
 
 
 def kernel(
-    starts, states, levels, states_v, energy, left_hbm, right_hbm, dens_hbm,
+    starts_hbm, states_hbm, levels_hbm, energy_hbm, left_hbm, right_hbm, dens_hbm,
     coup_ref, heff_ref,
-    lv, rv, dens, pick, gp, gz, acc_l, acc_t, part, cbuf, hbuf,
+    starts, states, levels, states_v, energy, lv, rv, dens, pick, gp, gz, acc_l, acc_t, part, cbuf, hbuf,
     load_sem, dens_send, dens_recv,
     zs_send, zs_recv, zp_send, zp_recv, p1_send, p1_recv, p2_send, p2_recv,
     c_send, c_recv, h_send, h_recv,
@@ -41,27 +43,32 @@
     def turn(v, by, n):
         return lax.rem(v + by + n, n)
 
-    loads = [
-        pltpu.make_async_copy(left_hbm, lv, load_sem.at[0]),
-        pltpu.make_async_copy(right_hbm, rv, load_sem.at[1]),
-        pltpu.make_async_copy(dens_hbm, dens.at[core], load_sem.at[2]),
-    ]
-    for c in loads:
-        c.start()
     barrier = pltpu.get_barrier_semaphore()
     up = at(y, x, turn(z, 1, LONG), core)
     down = at(y, x, turn(z, -1, LONG), core)
     other = at(y, x, z, 1 - core)
-    near = [up, down, other]
+    up2 = at(y, x, turn(z, 2, LONG), core)
+    down2 = at(y, x, turn(z, -2, LONG), core)
+    near = [up, down, up2, down2, other]
     near += [at(y, turn(x, j, SIDE), z, core) for j in (1, 2, 3)]
     near += [at(turn(y, j, SIDE), x, z, core) for j in (1, 2, 3)]
     for d in near:
         pl.semaphore_signal(barrier, inc=1, device_id=d, device_id_type=MESH)
 
-    loads[0].wait()
-    loads[1].wait()
+    loads = [
+        pltpu.make_async_copy(src, dst, load_sem.at[n])
+        for n, (src, dst) in enumerate((
+            (left_hbm, lv), (right_hbm, rv), (dens_hbm, dens.at[core]), (energy_hbm, energy),
+            (starts_hbm, starts), (states_hbm, states), (levels_hbm, levels), (states_hbm, states_v),
+        ))
+    ]
+    for n in (0, 1, 3, 4, 5, 6, 7, 2):
+        loads[n].start()
+
+    for n in (0, 1, 3):
+        loads[n].wait()
     eye = lax.broadcasted_iota(I32, (rows, rows), 0) == lax.broadcasted_iota(I32, (rows, rows), 1)
-    ecol = jnp.sum(jnp.where(eye, energy[...], 0.0), axis=1, keepdims=True)
+    ecol = jnp.sum(jnp.where(eye, energy[...].astype(F32).reshape(1, rows), 0.0), axis=1, keepdims=True)
     col = lax.broadcasted_iota(I32, (rows, LANES), 1)
     pad = jnp.zeros((rows, LANES - rest), F32)
 
@@ -86,21 +93,56 @@
             src_ref=src, dst_ref=dst, send_sem=ssem, recv_sem=rsem, device_id=dev, device_id_type=MESH
         )
 
+    ends = (8, 7)
+
     def slot_of(way, k):
-        return k if way == 0 else jnp.where(k == 0, 0, k + 8)
-
-    def stripe(way, k):
-        dst = slot_of(way, k + 1)
+        return k if way == 0 or k == 0 else k + 8
+
+    def stripe(way, k, hops):
+        dst = slot_of(way, k + hops)
+        dev = ((up, up2), (down, down2))[way][hops - 1]
         return send(
-            gp.at[slot_of(way, k), y, x], gp.at[dst, y, x],
-            zs_send.at[dst], zs_recv.at[dst], up if way == 0 else down,
+            gp.at[slot_of(way, k), y, x], gp.at[dst, y, x], zs_send.at[dst], zs_recv.at[dst], dev
         )
 
-    def lane(way, k):
-        dst = slot_of(way, k + 1)
+    def stripe_to(way, k):
+        hops = 2 - k % 2
+        return stripe(way, k - hops, hops)
+
+    def forward(way, k):
+        for hops in (2, 1):
+            if k + hops <= ends[way]:
+                stripe(way, k, hops).start()
+
+    def lane(way, k, hops, cut):
+        dst = slot_of(way, k + hops)
+        dev = ((up, up2), (down, down2))[way][hops - 1]
+        part_of = pl.ds(cut * (OWN // CUTS), OWN // CUTS)
         return send(
-            gz.at[slot_of(way, k)], gz.at[dst],
-            zp_send.at[dst], zp_recv.at[dst], up if way == 0 else down,
+            gz.at[slot_of(way, k), part_of], gz.at[dst, part_of],
+            zp_send.at[dst, cut], zp_recv.at[dst, cut], dev,
+        )
+
+    def lane_to(way, k, cut):
+        hops = 2 - k % 2
+        return lane(way, k - hops, hops, cut)
+
+    def lanes(k):
+        for cut in range(CUTS):
+            for way in (0, 1):
+                if 0 < k <= ends[way]:
+                    lane_to(way, k, cut).wait_recv()
+                if k + 2 <= ends[way]:
+                    lane(way, k, 2, cut).start()
+        for cut in range(CUTS):
+            for way in (0, 1):
+                if k + 1 <= ends[way]:
+                    lane(way, k, 1, cut).start()
+
+    def give(g):
+        part_of = pl.ds(g * (slots // GIVES), slots // GIVES)
+        return send(
+            dens_hbm.at[part_of], dens.at[core, part_of], dens_send.at[g], dens_recv.at[g], other
         )
 
     def first(way, k, j):
@@ -127,11 +169,11 @@
         return send(ref, ref, p2_send.at[s, j - 1], p2_recv.at[s, j - 1], other)
 
     for way in (0, 1):
-        stripe(way, 0).start()
-    for way in (0, 1):
-        lane(way, 0).start()
-    give = send(dens_hbm, dens.at[core], dens_send.at[0], dens_recv.at[0], other)
-    give.start()
+        forward(way, 0)
+    lanes(0)
+
+    for n in (4, 5, 6, 7):
+        loads[n].wait()
 
     ahead = lax.broadcasted_iota(I32, (rows, wide), 1) - lax.broadcasted_iota(I32, (rows, wide), 0)
 
@@ -143,57 +185,39 @@
     lax.fori_loop(0, 2 * slots, fill, 0)
     pick[2 * slots] = jnp.where(ahead == ntrip, 1.0, 0.0).astype(BF16)
 
-    def step(k, carry):
+    def plane_on(s):
+        for k in (2 * s - 1, 2 * s):
+            for way in (0, 1):
+                if k <= ends[way]:
+                    for j in (1, 2, 3):
+                        first_in(way, k, j).wait_recv()
+                    for j in (2, 1, 3):
+                        second(way, k, j).start()
+
+    for s in (1, 2, 3, 4):
+        for k in (2 * s - 1, 2 * s):
+            for way in (0, 1):
+                if k <= ends[way]:
+                    stripe_to(way, k).wait_recv()
+                    if k % 2 == 0:
+                        forward(way, k)
+                    for j in (2, 1, 3):
+                        first(way, k, j).start()
+        lanes(2 * s)
+        if s > 1:
+            plane_on(s - 1)
+        for g in range((s - 1) * GIVES // 4, s * GIVES // 4):
+            give(g).start()
+    plane_on(4)
+    for k in (1, 3, 5, 7):
         for way in (0, 1):
-            stripe(way, k - 1).wait_recv()
-            if way == 0:
-                stripe(way, k).start()
-            else:
-                @pl.when(k < 7)
-                def _():
-                    stripe(1, k).start()
-            for j in (2, 1, 3):
-                first(way, k, j).start()
-        for way in (0, 1):
-            lane(way, k - 1).wait_recv()
-            if way == 0:
-                lane(way, k).start()
-            else:
-                @pl.when(k < 7)
-                def _():
-                    lane(1, k).start()
-
-        @pl.when(k > 1)
-        def _():
-            for way in (0, 1):
-                for j in (1, 2, 3):
-                    first_in(way, k - 1, j).wait_recv()
-                for j in (2, 1, 3):
-                    second(way, k - 1, j).start()
-        return carry
-
-    lax.fori_loop(1, 8, step, 0)
-    stripe(0, 7).wait_recv()
-    for j in (2, 1, 3):
-        first(0, 8, j).start()
-    for way, k in ((0, 7), (1, 7), (0, 8)):
-        for j in (1, 2, 3):
-            first_in(way, k, j).wait_recv()
-        for j in (2, 1, 3):
-            second(way, k, j).start()
-    lane(0, 7).wait_recv()
-
-    def arrived(k, carry):
-        for way in (0, 1):
-            for j in (1, 2, 3):
-                second_in(way, k, j).wait_recv()
-        return carry
-
-    lax.fori_loop(1, 8, arrived, 0)
-    for j in (1, 2, 3):
-        second_in(0, 8, j).wait_recv()
+            for cut in range(CUTS):
+                lane_to(way, k, cut).wait_recv()
     loads[2].wait()
-    give.wait_recv()
+    for g in range(GIVES):
+        give(g).wait_recv()
+
+    alone = (2 * SIDE * SIDE - tiles) // 2
 
     def two(t):
         halves = []
@@ -205,24 +229,43 @@
             halves.append(v.reshape(LONG * rows, LANES))
         return jnp.concatenate(halves, axis=1)
 
+    half = slots * rows
+
+    def add(acc, lo, got, fresh):
+        if fresh:
+            acc[lo : lo + got.shape[0], :] = got
+        else:
+            acc[lo : lo + got.shape[0], :] += got
+
+    def contract(m, fresh):
+        b = two(tiles + 2 * m)
+        for h in (0, 1):
+            if m < tiles // 2 - 1:
+                d = dens[h, :, :, 2 * m * LANES : 2 * (m + 1) * LANES].reshape(half, 2 * LANES)
+            else:
+                d = dens[h, :, :, 2 * m * LANES : ntrip].reshape(half, ntrip - 2 * m * LANES)
+                d = jnp.concatenate([d, jnp.zeros((half, wide - ntrip), BF16)], axis=1)
+            add(acc_t, h * half, nt(d, b), fresh)
+
+    def select(m, fresh):
+        cols = slice(2 * m * LANES, 2 * (m + 1) * LANES)
+        b = two(2 * m)
+        for h in (0, 1):
+            lo, hi = h * slots, (h + 1) * slots + h
+            d = pick[lo:hi, :, cols].reshape((hi - lo) * rows, 2 * LANES)
+            add(acc_l, lo * rows, nt(d, b), fresh)
+
+    for m in range(alone, tiles // 2):
+        contract(m, m == alone)
+    for k in range(1, 9):
+        for way in (0, 1):
+            if k <= ends[way]:
+                for j in (1, 2, 3):
+                    second_in(way, k, j).wait_recv()
     for m in range(tiles // 2):
-        cols = slice(2 * m * LANES, 2 * (m + 1) * LANES)
-        got = nt(pick[:, :, cols].reshape((2 * slots + 1) * rows, 2 * LANES), two(2 * m))
-        if m == 0:
-            acc_l[...] = got
-        else:
-            acc_l[...] += got
-    for m in range(tiles // 2):
-        if m < tiles // 2 - 1:
-            d = dens[:, :, :, 2 * m * LANES : 2 * (m + 1) * LANES].reshape(2 * slots * rows, 2 * LANES)
-        else:
-            d = dens[:, :, :, 2 * m * LANES : ntrip].reshape(2 * slots * rows, ntrip - 2 * m * LANES)
-            d = jnp.concatenate([d, jnp.zeros((2 * slots * rows, wide - ntrip), BF16)], axis=1)
-        got = nt(d, two(tiles + 2 * m))
-        if m == 0:
-            acc_t[...] = got
-        else:
-            acc_t[...] += got
+        select(m, m == 0)
+    for m in range(alone):
+        contract(m, False)
 
     erow = jnp.broadcast_to(acc_l[2 * slots * rows : 2 * slots * rows + 1, :], (8, LONG * rows))
 
@@ -291,23 +334,17 @@
     for j in range(1, np_):
         plane(j).start()
 
-    give.wait_send()
-
-    def left(k, carry):
+    for g in range(GIVES):
+        give(g).wait_send()
+    for k in range(1, 9):
         for way in (0, 1):
-            stripe(way, k - 1).wait_send()
-            lane(way, k - 1).wait_send()
-            for j in (1, 2, 3):
-                first(way, k, j).wait_send()
-                second(way, k, j).wait_send()
-        return carry
-
-    lax.fori_loop(1, 8, left, 0)
-    stripe(0, 7).wait_send()
-    lane(0, 7).wait_send()
-    for j in (1, 2, 3):
-        first(0, 8, j).wait_send()
-        second(0, 8, j).wait_send()
+            if k <= ends[way]:
+                stripe_to(way, k).wait_send()
+                for cut in range(CUTS):
+                    lane_to(way, k, cut).wait_send()
+                for j in (1, 2, 3):
+                    first(way, k, j).wait_send()
+                    second(way, k, j).wait_send()
 
     def gone(j, carry):
         couplings(j).wait_send()
@@ -332,15 +369,19 @@
     slots, rows, ntrip = density.shape
     n = rows * LONG
     wide = -(-ntrip // LANES) * LANES
-    smem, vmem, hbm = (pl.BlockSpec(memory_space=m) for m in (pltpu.SMEM, pltpu.VMEM, pl.ANY))
-    dma, reg = pltpu.SemaphoreType.DMA, pltpu.SemaphoreType.REGULAR
-    pair_states = states.T
+    vmem, hbm = (pl.BlockSpec(memory_space=m) for m in (pltpu.VMEM, pl.ANY))
+    dma = pltpu.SemaphoreType.DMA
     couplings, heff = pl.pallas_call(
         kernel,
         out_shape=(jax.ShapeDtypeStruct((1, slots), F32), jax.ShapeDtypeStruct((8, 8), F32)),
-        in_specs=[smem, smem, smem, vmem, vmem, hbm, hbm, hbm],
+        in_specs=[hbm] * 7,
         out_specs=(vmem, vmem),
         scratch_shapes=[
+            pltpu.SMEM((slots,), I32),
+            pltpu.SMEM((2, slots), I32),
+            pltpu.SMEM((8,), F32),
+            pltpu.VMEM((2, slots), I32),
+            pltpu.VMEM((rows,), BF16),
             pltpu.VMEM((rows, ntrip), BF16),
             pltpu.VMEM((rows, ntrip), BF16),
             pltpu.VMEM((2, slots, rows, ntrip), BF16),
@@ -352,17 +393,16 @@
             pltpu.VMEM((slots, 8, LANES), F32),
             pltpu.VMEM((2 * LONG, 1, LANES), F32),
             pltpu.VMEM((SIDE * SIDE, 8, LANES), F32),
-            dma((3,)), dma((1,)), dma((1,)),
-            dma((LONG,)), dma((LONG,)), dma((LONG,)), dma((LONG,)),
+            dma((8,)), dma((GIVES,)), dma((GIVES,)),
+            dma((LONG,)), dma((LONG,)), dma((LONG, CUTS)), dma((LONG, CUTS)),
             dma((LONG, 3)), dma((LONG, 3)), dma((LONG, 3)), dma((LONG, 3)),
             dma((2 * LONG,)), dma((2 * LONG,)), dma((SIDE * SIDE,)), dma((SIDE * SIDE,)),
         ],
         compiler_params=pltpu.CompilerParams(
-            collective_id=0, has_side_effects=True, vmem_limit_bytes=52 * 1024 * 1024
+            collective_id=0, has_side_effects=True, vmem_limit_bytes=67043328
         ),
     )(
-        starts, pair_states, levels, pair_states, energy.astype(F32).reshape(1, rows),
-        left, right, density,
+        starts, states.T, levels, energy, left, right, density,
     )
     return couplings.reshape(slots), heff
 

time: 71.7 us -> 60.5 us (0.84)
  Pallas kernels: 65.3 us -> 57.3 us
  local copies, waits for them, and re-layouts: 4.87 us -> 2.4 us
    pallas_call x1, Pallas kernels: 65.3 us -> 57.3 us  [local(): pl.pallas_call(kernel, out_shape=(jax.ShapeDtypeStruct((1, slots), F32),...]
    unnamed x12 -> x2, local copies, waits for them, and re-layouts: 4.87 us -> 2.4 us
where the time goes in v2:
time: 60.5 us; the launch traced here: 60.4 us
  Pallas kernels  57.3 us (95%)
  local copies, waits for them, and re-layouts  2.4 us (4%)
  between operations  0.64 us (1%)
    pallas_call x1, Pallas kernels, local(): pl.pallas_call(kernel, out_shape=(jax.ShapeDtypeStruct((1, slots), F32),...  57.3 us
    unnamed x2, local copies, waits for them, and re-layouts  2.4 us

profile of v2, /device:TPU:1, one launch (start us, length us, event | category | flops | bytes accessed | tf_op | source)
XLA Modules:
  0.0 60.4 jit_solution(732125058996829407)
XLA Ops:
  0.6 57.3 %shard_map.86 = (f32[1,40]{1,0:T(1,128)}, f32[8,8]{1,0:T(8,128)}) custom-call(s32[40]{0:T(128)} %starts_hbm.1, s32[2,40]{1,0:T(2,128)} %bitcast.2, f32[8]{0:T(128)} %levels_hbm.1, bf16[16]{0:T(256)(128)(2,1)} %energy_hbm.1, bf16[16,2744]{1,0:T(8,128)(2,1)} %left_hbm.1, bf16[16,2744]{1,0:T(8,128)(2,1)} %right_hbm.1, bf16[40,16,2744]{2,1,0:T(8,128)(2,1)} %dens_hbm.1), custom_call_target="tpu_custom_call" | custom-call | tf_op jit(solution)/shard_map/pallas_call | solution.py:374
  58.0 1.1 %copy.11 = f32[40]{0:T(128)} copy(f32[40]{0:T(128)} %bitcast.3) | data formatting | bytes 320
  59.1 1.3 %copy.12 = f32[8,8]{1,0:T(8,128)} copy(f32[8,8]{1,0:T(8,128)} %get-tuple-element.9) | data formatting | bytes 512

commit v3 on v2

--- a/solution.py
+++ b/solution.py
@@ -23,9 +23,7 @@
     starts_hbm, states_hbm, levels_hbm, energy_hbm, left_hbm, right_hbm, dens_hbm,
     coup_ref, heff_ref,
     starts, states, levels, states_v, energy, lv, rv, dens, pick, gp, gz, acc_l, acc_t, part, cbuf, hbuf,
-    load_sem, dens_send, dens_recv,
-    zs_send, zs_recv, zp_send, zp_recv, p1_send, p1_recv, p2_send, p2_recv,
-    c_send, c_recv, h_send, h_recv,
+    load_sem, send_sem, dens_recv, zs_recv, zp_recv, odd_recv, p1_recv, p2_recv, c_recv, h_recv,
 ):
     slots, rows, ntrip = dens_hbm.shape
     tiles = -(-ntrip // LANES)
@@ -93,6 +91,10 @@
             src_ref=src, dst_ref=dst, send_sem=ssem, recv_sem=rsem, device_id=dev, device_id_type=MESH
         )
 
+    def bytes_of(ref, sem):
+        pltpu.make_async_copy(ref, ref, sem).wait()
+
+    STRIPE, LANE, FIRST, SECOND, DENS, COUPLE, HEFF = (send_sem.at[n] for n in range(7))
     ends = (8, 7)
 
     def slot_of(way, k):
@@ -102,7 +104,7 @@
         dst = slot_of(way, k + hops)
         dev = ((up, up2), (down, down2))[way][hops - 1]
         return send(
-            gp.at[slot_of(way, k), y, x], gp.at[dst, y, x], zs_send.at[dst], zs_recv.at[dst], dev
+            gp.at[slot_of(way, k), y, x], gp.at[dst, y, x], STRIPE, zs_recv.at[dst], dev
         )
 
     def stripe_to(way, k):
@@ -118,20 +120,14 @@
         dst = slot_of(way, k + hops)
         dev = ((up, up2), (down, down2))[way][hops - 1]
         part_of = pl.ds(cut * (OWN // CUTS), OWN // CUTS)
-        return send(
-            gz.at[slot_of(way, k), part_of], gz.at[dst, part_of],
-            zp_send.at[dst, cut], zp_recv.at[dst, cut], dev,
-        )
-
-    def lane_to(way, k, cut):
-        hops = 2 - k % 2
-        return lane(way, k - hops, hops, cut)
+        sem = zp_recv.at[(k + hops) // 2 - 1, way, cut] if hops == 2 else odd_recv.at[0]
+        return send(gz.at[slot_of(way, k), part_of], gz.at[dst, part_of], LANE, sem, dev)
 
     def lanes(k):
         for cut in range(CUTS):
             for way in (0, 1):
                 if 0 < k <= ends[way]:
-                    lane_to(way, k, cut).wait_recv()
+                    lane(way, k - 2, 2, cut).wait_recv()
                 if k + 2 <= ends[way]:
                     lane(way, k, 2, cut).start()
         for cut in range(CUTS):
@@ -142,13 +138,13 @@
     def give(g):
         part_of = pl.ds(g * (slots // GIVES), slots // GIVES)
         return send(
-            dens_hbm.at[part_of], dens.at[core, part_of], dens_send.at[g], dens_recv.at[g], other
+            dens_hbm.at[part_of], dens.at[core, part_of], DENS, dens_recv.at[0], other
         )
 
     def first(way, k, j):
         s = slot_of(way, k)
         dev = at(y, turn(x, j, SIDE), z, core) if way == 0 else at(turn(y, j, SIDE), x, z, core)
-        return send(gp.at[s, y, x], gp.at[s, y, x], p1_send.at[s, j - 1], p1_recv.at[s, j - 1], dev)
+        return send(gp.at[s, y, x], gp.at[s, y, x], FIRST, p1_recv.at[s], dev)
 
     def second(way, k, j):
         s = slot_of(way, k)
@@ -156,21 +152,19 @@
             ref, dev = gp.at[s, y], at(turn(y, j, SIDE), x, z, core)
         else:
             ref, dev = gp.at[s, :, x], at(y, turn(x, j, SIDE), z, core)
-        return send(ref, ref, p2_send.at[s, j - 1], p2_recv.at[s, j - 1], dev)
-
-    def first_in(way, k, j):
-        s = slot_of(way, k)
-        ref = gp.at[s, y, turn(x, -j, SIDE)] if way == 0 else gp.at[s, turn(y, -j, SIDE), x]
-        return send(ref, ref, p1_send.at[s, j - 1], p1_recv.at[s, j - 1], other)
-
-    def second_in(way, k, j):
-        s = slot_of(way, k)
-        ref = gp.at[s, turn(y, -j, SIDE)] if way == 0 else gp.at[s, :, turn(x, -j, SIDE)]
-        return send(ref, ref, p2_send.at[s, j - 1], p2_recv.at[s, j - 1], other)
+        return send(ref, ref, SECOND, p2_recv.at[0], dev)
+
+    def first_in(way, k):
+        bytes_of(gp.at[slot_of(way, k), 0, 0:3], p1_recv.at[slot_of(way, k)])
+
+    def give_some(n):
+        for g in range(n * GIVES // 4, (n + 1) * GIVES // 4):
+            give(g).start()
 
     for way in (0, 1):
         forward(way, 0)
     lanes(0)
+    give_some(0)
 
     for n in (4, 5, 6, 7):
         loads[n].wait()
@@ -186,16 +180,15 @@
     pick[2 * slots] = jnp.where(ahead == ntrip, 1.0, 0.0).astype(BF16)
 
     def plane_on(s):
-        for k in (2 * s - 1, 2 * s):
+        for k in (2 * s, 2 * s - 1):
             for way in (0, 1):
                 if k <= ends[way]:
-                    for j in (1, 2, 3):
-                        first_in(way, k, j).wait_recv()
+                    first_in(way, k)
                     for j in (2, 1, 3):
                         second(way, k, j).start()
 
     for s in (1, 2, 3, 4):
-        for k in (2 * s - 1, 2 * s):
+        for k in (2 * s, 2 * s - 1):
             for way in (0, 1):
                 if k <= ends[way]:
                     stripe_to(way, k).wait_recv()
@@ -203,19 +196,16 @@
                         forward(way, k)
                     for j in (2, 1, 3):
                         first(way, k, j).start()
-        lanes(2 * s)
         if s > 1:
             plane_on(s - 1)
-        for g in range((s - 1) * GIVES // 4, s * GIVES // 4):
-            give(g).start()
+        if s < 4:
+            lanes(2 * s)
+            give_some(s)
     plane_on(4)
-    for k in (1, 3, 5, 7):
-        for way in (0, 1):
-            for cut in range(CUTS):
-                lane_to(way, k, cut).wait_recv()
+    lanes(8)
+    bytes_of(gz.at[0:8], odd_recv.at[0])
     loads[2].wait()
-    for g in range(GIVES):
-        give(g).wait_recv()
+    bytes_of(dens.at[0], dens_recv.at[0])
 
     alone = (2 * SIDE * SIDE - tiles) // 2
 
@@ -257,11 +247,7 @@
 
     for m in range(alone, tiles // 2):
         contract(m, m == alone)
-    for k in range(1, 9):
-        for way in (0, 1):
-            if k <= ends[way]:
-                for j in (1, 2, 3):
-                    second_in(way, k, j).wait_recv()
+    bytes_of(gp.at[1:LONG, :, 0:3], p2_recv.at[0])
     for m in range(tiles // 2):
         select(m, m == 0)
     for m in range(alone):
@@ -287,24 +273,13 @@
 
     nv = 2 * LONG
 
-    def couplings(j):
+    def go(j, carry):
         dev = (pair, lax.rem(virt + j, nv))
-        return send(cbuf.at[virt], cbuf.at[virt], c_send.at[j], c_recv.at[j], dev)
-
-    def couplings_in(j):
-        ref = cbuf.at[lax.rem(virt + nv - j, nv)]
-        return send(ref, ref, c_send.at[j], c_recv.at[j], other)
-
-    def go(j, carry):
-        couplings(j).start()
+        send(cbuf.at[virt], cbuf.at[virt], COUPLE, c_recv.at[0], dev).start()
         return carry
 
-    def come(j, carry):
-        couplings_in(j).wait_recv()
-        return carry
-
-    lax.fori_loop(1, nv, go, 0)
-    lax.fori_loop(1, nv, come, 0)
+    lax.fori_loop(1, nv, go, 0, unroll=True)
+    bytes_of(cbuf.at[1:nv], c_recv.at[0])
     total = jnp.sum(cbuf[...], axis=0)
     coup_ref[...] = total[:, :slots]
 
@@ -323,37 +298,18 @@
     hbuf[pair] = local
     np_ = SIDE * SIDE
 
-    def plane(j):
+    for j in range(1, np_):
         dev = (lax.rem(pair + j, np_), virt)
-        return send(hbuf.at[pair], hbuf.at[pair], h_send.at[j], h_recv.at[j], dev)
-
-    def plane_in(j):
-        ref = hbuf.at[lax.rem(pair + np_ - j, np_)]
-        return send(ref, ref, h_send.at[j], h_recv.at[j], other)
-
-    for j in range(1, np_):
-        plane(j).start()
-
-    for g in range(GIVES):
-        give(g).wait_send()
-    for k in range(1, 9):
-        for way in (0, 1):
-            if k <= ends[way]:
-                stripe_to(way, k).wait_send()
-                for cut in range(CUTS):
-                    lane_to(way, k, cut).wait_send()
-                for j in (1, 2, 3):
-                    first(way, k, j).wait_send()
-                    second(way, k, j).wait_send()
-
-    def gone(j, carry):
-        couplings(j).wait_send()
-        return carry
-
-    lax.fori_loop(1, nv, gone, 0)
-
-    for j in range(1, np_):
-        plane_in(j).wait_recv()
+        send(hbuf.at[pair], hbuf.at[pair], HEFF, h_recv.at[0], dev).start()
+
+    bytes_of(gp.at[1:LONG, 0, 0], STRIPE)
+    bytes_of(gz.at[1:LONG], LANE)
+    bytes_of(gp.at[1:LONG, 0, 0:3], FIRST)
+    bytes_of(gp.at[1:LONG, :, 0:3], SECOND)
+    bytes_of(dens.at[0], DENS)
+    bytes_of(cbuf.at[1:nv], COUPLE)
+
+    bytes_of(hbuf.at[1:np_], h_recv.at[0])
     square = jnp.sum(hbuf[...], axis=0)[:, :8]
     one = lax.broadcasted_iota(I32, (8, 8), 0)
     two_ = lax.broadcasted_iota(I32, (8, 8), 1)
@@ -361,15 +317,14 @@
     for n in range(8):
         out += jnp.where((one == n) & (two_ == n), levels[n], 0.0)
     heff_ref[...] = out
-    for j in range(1, np_):
-        plane(j).wait_send()
+    bytes_of(hbuf.at[1:np_], HEFF)
 
 
 def local(density, left, right, energy, levels, states, starts):
     slots, rows, ntrip = density.shape
     n = rows * LONG
     wide = -(-ntrip // LANES) * LANES
-    vmem, hbm = (pl.BlockSpec(memory_space=m) for m in (pltpu.VMEM, pl.ANY))
+    vmem, hbm = (pl.BlockSpec(memory_space=m) for m in (pltpu.VMEM, pltpu.HBM))
     dma = pltpu.SemaphoreType.DMA
     couplings, heff = pl.pallas_call(
         kernel,
@@ -393,10 +348,8 @@
             pltpu.VMEM((slots, 8, LANES), F32),
             pltpu.VMEM((2 * LONG, 1, LANES), F32),
             pltpu.VMEM((SIDE * SIDE, 8, LANES), F32),
-            dma((8,)), dma((GIVES,)), dma((GIVES,)),
-            dma((LONG,)), dma((LONG,)), dma((LONG, CUTS)), dma((LONG, CUTS)),
-            dma((LONG, 3)), dma((LONG, 3)), dma((LONG, 3)), dma((LONG, 3)),
-            dma((2 * LONG,)), dma((2 * LONG,)), dma((SIDE * SIDE,)), dma((SIDE * SIDE,)),
+            dma((8,)), dma((7,)), dma((1,)), dma((LONG,)), dma((4, 2, CUTS)), dma((1,)),
+            dma((LONG,)), dma((1,)), dma((1,)), dma((1,)),
         ],
         compiler_params=pltpu.CompilerParams(
             collective_id=0, has_side_effects=True, vmem_limit_bytes=67043328

time: 60.5 us -> 55.8 us (0.922)
  Pallas kernels: 57.3 us -> 52.6 us
    pallas_call x1, Pallas kernels: 57.3 us -> 52.6 us  [local(): pl.pallas_call(kernel, out_shape=(jax.ShapeDtypeStruct((1, slots), F32),...]
where the time goes in v3:
time: 55.8 us; the launch traced here: 55.7 us
  Pallas kernels  52.6 us (94%)
  local copies, waits for them, and re-layouts  2.4 us (4%)
  between operations  0.64 us (1%)
    pallas_call x1, Pallas kernels, local(): pl.pallas_call(kernel, out_shape=(jax.ShapeDtypeStruct((1, slots), F32),...  52.6 us
    unnamed x2, local copies, waits for them, and re-layouts  2.4 us

profile of v3, /device:TPU:1, one launch (start us, length us, event | category | flops | bytes accessed | tf_op | source)
XLA Modules:
  0.0 55.7 jit_solution(7152244939930617869)
XLA Ops:
  0.6 52.6 %shard_map.86 = (f32[1,40]{1,0:T(1,128)}, f32[8,8]{1,0:T(8,128)}) custom-call(s32[40]{0:T(128)} %starts_hbm.1, s32[2,40]{1,0:T(2,128)} %bitcast.2, f32[8]{0:T(128)} %levels_hbm.1, bf16[16]{0:T(256)(128)(2,1)} %energy_hbm.1, bf16[16,2744]{1,0:T(8,128)(2,1)} %left_hbm.1, bf16[16,2744]{1,0:T(8,128)(2,1)} %right_hbm.1, bf16[40,16,2744]{2,1,0:T(8,128)(2,1)} %dens_hbm.1), custom_call_target="tpu_custom_call" | custom-call | tf_op jit(solution)/shard_map/pallas_call | solution.py:329
  53.3 1.1 %copy.11 = f32[40]{0:T(128)} copy(f32[40]{0:T(128)} %bitcast.3) | data formatting | bytes 320
  54.4 1.3 %copy.12 = f32[8,8]{1,0:T(8,128)} copy(f32[8,8]{1,0:T(8,128)} %get-tuple-element.9) | data formatting | bytes 512
